TPU v7x, 16 devices: a whole 2x2x2 slice. The times are simulated.
16 devices in a mesh: by: 2 (over z), bx: 8 (over y, x, core).
Axes of the slice: x: 2, y: 2, z: 2, core: 2. Of those that a mesh axis runs over, the one named last changes fastest.
Arguments:
- wave_fn: float32 [3072, 2, 2, 3072], P('bx', None, None, 'by')
- left_env: float32 [3072, 3, 3072], P('bx')
- mpo_ten: float32 [3, 2, 2, 3], replicated
- right_env: float32 [3072, 3, 3072], P('by')
Outputs:
- output: float32 [3072, 2, 2, 3072], P('bx', None, None, 'by')
All inputs are finite; a program needn't handle non-finite values.
Results may differ from a plain program's by a relative error of at most 0.001.
Values sent between devices are 32-bit elements.
A program may use at most 1 GiB of HBM per device.

v0:
```python
import jax
import jax.numpy as jnp
from jax import lax
from jax.sharding import PartitionSpec as P


def solution(mesh):
    prec_mode = lax.Precision.HIGHEST

    def local_apply(wave_blk, left_rows, mpo_ten, right_rows):
        row_share, mpo_dim, bond_dim = left_rows.shape
        phys_dim = wave_blk.shape[1]
        col_share = wave_blk.shape[3]
        wave_cols = lax.all_gather(wave_blk, 'bx', axis=0, tiled=True)
        stage_one = jnp.dot(left_rows.reshape(row_share * mpo_dim, bond_dim), wave_cols.reshape(bond_dim, phys_dim * phys_dim * col_share), precision=prec_mode, preferred_element_type=jnp.float32)
        stage_one = stage_one.reshape(row_share, mpo_dim, phys_dim, phys_dim, col_share)
        stage_two = jnp.einsum('aupqf,uspv->asvqf', stage_one, mpo_ten, precision=prec_mode, preferred_element_type=jnp.float32)
        stage_three = jnp.einsum('asvqf,vtqr->astrf', stage_two, mpo_ten, precision=prec_mode, preferred_element_type=jnp.float32)
        right_cols = lax.all_to_all(right_rows, 'by', 2, 0, tiled=True)
        part_sum = lax.dot_general(stage_three.reshape(row_share * phys_dim * phys_dim, mpo_dim * col_share), right_cols.reshape(bond_dim, mpo_dim * col_share), (((1,), (1,)), ((), ())), precision=prec_mode, preferred_element_type=jnp.float32)
        part_sum = part_sum.reshape(row_share, phys_dim, phys_dim, bond_dim)
        return lax.psum_scatter(part_sum, 'by', scatter_dimension=3, tiled=True)

    return jax.shard_map(local_apply, mesh=mesh, in_specs=(P('bx', None, None, 'by'), P('bx', None, None), P(), P('by', None, None)), out_specs=P('bx', None, None, 'by'), check_vma=False)
```

profile of v0, /device:TPU:0, one launch (start us, length us, event | category | flops | bytes accessed | tf_op | source)
XLA Modules:
  0.0 2191.0 jit_solution(7544649531766312825)
XLA Ops:
  6.5 0.0 copy-start
  6.5 0.0 all-gather.2.cloned.1.call-start
  6.5 0.7 all-gather.2.cloned.1.call-update
  7.3 79.9 %copy.20 = f32[1536,3,3072]{0,1,2:T(4,128)} copy(f32[1536,3,3072]{2,0,1:T(8,128)} %param.7) | data formatting | bytes 113246208 | tf_op args[3]
  87.1 26.6 %all-to-all-start = ((f32[1536,3,3072]{0,1,2:T(4,128)}), f32[1536,3,3072]{0,1,2:T(4,128)}, u32[]{:S(2)}, u32[]{:S(2)}) async-start(f32[1536,3,3072]{0,1,2:T(4,128)} %copy.20), calls=%async_computation | async-start | bytes 150994944 | tf_op jit(solution)/shard_map/all_to_all | solution.py:19
  113.7 0.0 reduce-scatter.2.cloned.1.call-start
  113.8 0.0 copy-done
  113.8 0.6 fusion.25
  114.4 812.2 %all-to-all-done = f32[1536,3,3072]{0,1,2:T(4,128)} async-done(((f32[1536,3,3072]{0,1,2:T(4,128)}), f32[1536,3,3072]{0,1,2:T(4,128)}, u32[]{:S(2)}, u32[]{:S(2)}) %all-to-all-start) | async-done | bytes 56623136 | tf_op jit(solution)/shard_map/all_to_all | solution.py:19
  926.6 78.0 %copy.21 = f32[1536,3,2,1536]{0,2,3,1:T(2,128)} copy(f32[1536,3,2,1536]{0,1,3,2:T(4,128)} %bitcast.18) | data formatting | bytes 113246208 | tf_op jit(solution)/shard_map/all_to_all | solution.py:19
  1004.6 37.9 %copy.42 = f32[576,8,2,1536]{3,1,2,0:T(8,128)} copy(f32[576,8,2,1536]{3,2,1,0:T(2,128)} %bitcast.57) | data formatting | bytes 113246208
  1042.6 0.0 all-gather.2.cloned.1.call-done
  1042.6 108.0 %copy.34 = f32[3072,2,2,1536]{0,3,2,1:T(8,128)} copy(f32[3072,2,2,1536]{3,2,1,0:T(2,128)} %all-gather.2.cloned.1.call-done) | data formatting | bytes 150994944 | tf_op jit(solution)/shard_map/reshape | solution.py:15
  1150.5 0.0 copy-start.1
  1150.5 283.4 %fusion.11 = f32[384,3,2,2,1536,1]{4,0,3,2,1,5:T(8,128)} fusion(f32[3072,2,2,1536]{0,3,2,1:T(8,128)} %copy.34, f32[384,3,3072]{2,0,1:T(8,128)} %param.5), kind=kOutput, calls=%fused_computation.9 | convolution fusion | flops 260919263232 | bytes 117964800 | tf_op jit(solution)/shard_map/dot_general | solution.py:15
  1434.0 0.0 copy-done.1
  1434.0 122.8 %fusion.6 = f32[384,2,1536,2,3,1]{2,4,5,1,3,0:T(4,128)} fusion(f32[384,3,2,2,1536,1]{4,0,3,2,1,5:T(8,128)} %fusion.11, f32[3,2,2,3,1,1]{3,2,0,5,1,4:T(2,128)S(1)} %copy-done.1), kind=kOutput, calls=%fused_computation.6 | convolution fusion | flops 509607936 | bytes 56623248 | tf_op jit(solution)/shard_map/aupqf,uspv->asvqf/dot_general | solution.py:17
  1556.8 82.8 %fusion.8 = f32[384,2,2,3,1536]{4,3,2,1,0:T(4,128)} fusion(f32[384,2,1536,2,3,1]{2,4,5,1,3,0:T(4,128)} %fusion.6, f32[3,2,2,3,1,1]{3,2,1,0,5,4:T(2,128)S(1)} %bitcast.56), kind=kOutput, calls=%fused_computation.8 | convolution fusion | flops 509607936 | bytes 56623248 | tf_op jit(solution)/shard_map/asvqf,vtqr->astrf/dot_general | solution.py:18
  1639.7 38.9 %copy.19 = f32[384,2,2,3,1536]{0,4,3,2,1:T(8,128)} copy(f32[384,2,2,3,1536]{4,3,2,1,0:T(4,128)} %fusion.8) | data formatting | bytes 56623104 | tf_op jit(solution)/shard_map/asvqf,vtqr->astrf/transpose | solution.py:18
  1678.5 278.1 %fusion.2 = f32[384,2,2,3072]{3,0,2,1:T(8,128)} fusion(f32[384,2,2,4608]{0,3,2,1:T(8,128)} %bitcast.59, f32[3072,4608]{0,1:T(8,128)} %bitcast.58), kind=kOutput, calls=%fused_computation.2 | convolution fusion | flops 260919263232 | bytes 103809024 | tf_op jit(solution)/shard_map/dot_general | solution.py:20
  1956.7 0.0 reduce-scatter.2.cloned.1.call-update
  1956.7 210.2 %reduce-scatter.2.cloned.1.call-done = f32[384,2,2,1536]{3,0,2,1:T(8,128)} async-done(((f32[384,2,2,3072]{3,0,2,1:T(8,128)}), f32[384,2,2,1536]{3,0,2,1:T(8,128)}) %reduce-scatter.2.cloned.1.call-update) | async-done | bytes 9437200 | tf_op jit(solution)/shard_map/reduce_scatter | solution.py:22
  2166.9 17.1 copy.24
Async XLA Ops:
  6.5 107.3 %copy-start = (f32[3,2,2,3]{3,2,1,0:T(2,128)S(1)}, f32[3,2,2,3]{3,2,1,0:T(2,128)}, u32[]{:S(2)}) copy-start(f32[3,2,2,3]{3,2,1,0:T(2,128)} %param.6) | copy-start | bytes 436
  6.5 1036.0 %all-gather.2.cloned.1.call-start = ((), (), s32[]{:S(2)}) async-start(), calls=%async_computation.2 | async-start | bytes 84934656 | tf_op jit(solution)/shard_map/all_gather | solution.py:14
  87.1 839.5 %all-to-all-start = ((f32[1536,3,3072]{0,1,2:T(4,128)}), f32[1536,3,3072]{0,1,2:T(4,128)}, u32[]{:S(2)}, u32[]{:S(2)}) async-start(f32[1536,3,3072]{0,1,2:T(4,128)} %copy.20), calls=%async_computation | async-start | bytes 150994944 | tf_op jit(solution)/shard_map/all_to_all | solution.py:19
  113.7 2053.1 %reduce-scatter.2.cloned.1.call-start = ((), (), s32[]{:S(2)}) async-start(), calls=%async_computation.3 | async-start | bytes 28311552 | tf_op jit(solution)/shard_map/reduce_scatter | solution.py:22
  1150.5 283.4 %copy-start.1 = (f32[3,2,2,3,1,1]{3,2,0,5,1,4:T(2,128)S(1)}, f32[3,2,2,3,1,1]{3,2,0,5,1,4:T(2,128)}, u32[]{:S(2)}) copy-start(f32[3,2,2,3,1,1]{3,2,0,5,1,4:T(2,128)} %fusion.25) | copy-start | bytes 436
Sparse Core Ops, SparseCore 0:
  9.2 338.1 all-gather.1
  1956.8 210.0 reduce-scatter.1
where the time goes:
time: 2200 us; the launch traced here: 2190 us
  waiting for transfers between devices  1020 us (46%)
  matrix products  767 us (35%)
  local copies, waits for them, and re-layouts  360 us (16%)
  starting transfers between devices  26.6 us (1%)
    all_to_all x1, waiting for transfers between devices, local_apply(): right_cols = lax.all_to_all(right_rows, 'by', 2, 0, tiled=True)  812 us
    dot_general x1, matrix products, local_apply(): jnp.dot(left_rows.reshape(row_share * mpo_dim, bond_dim), wave_cols.resha...  283 us
    dot_general x1, matrix products, local_apply(): lax.dot_general(stage_three.reshape(row_share * phys_dim * phys_dim, mpo_...  278 us
    reduce_scatter x1, waiting for transfers between devices, local_apply(): return lax.psum_scatter(part_sum, 'by', scatter_dimension=3, tiled=True)  210 us
    dot_general x1, matrix products, local_apply(): jnp.einsum('aupqf,uspv->asvqf', stage_one, mpo_ten, precision=prec_mode,...  123 us
    unnamed x6, local copies, waits for them, and re-layouts  118 us
    reshape x1, local copies, waits for them, and re-layouts, local_apply(): wave_cols.reshape(bond_dim, phys_dim * phys_dim * col_share)  108 us
    dot_general x1, matrix products, local_apply(): jnp.einsum('asvqf,vtqr->astrf', stage_two, mpo_ten, precision=prec_mode,...  82.8 us
  transfers between devices with their start and end apart: 3, of which 2 were waited for; matrix products, arithmetic and copies ran while one was open for 9% of the time, Pallas kernels for 0%

commit v1 on v0

v1 whole, which is shorter than its diff:
```python
import functools
import jax
import jax.numpy as jnp
from jax import lax
from jax.experimental import pallas as pl
from jax.experimental.pallas import tpu as pltpu
from jax.sharding import PartitionSpec as P

MESH = pl.DeviceIdType.MESH
BF, F32 = jnp.bfloat16, jnp.float32
FB = 256
BT = 512

OWN, XN, YN, DN = 0, 1, 2, 3
UNITS = [(OWN, k) for k in range(6)]
UNITS += [(XN, 0), (YN, 0), (XN, 1), (YN, 1), (DN, 0)]
for _k in range(2, 6):
    UNITS += [(XN, _k), (YN, _k), (DN, _k - 1)]
UNITS += [(DN, 5)]


def split3(v):
    hi = v.astype(BF)
    rest = v - hi.astype(F32)
    mid = rest.astype(BF)
    low = (rest - mid.astype(F32)).astype(BF)
    return hi, mid, low


def dot6(a, b, rhs_dim):
    def d(i, j):
        return lax.dot_general(a[i], b[j], (((1,), (rhs_dim,)), ((), ())), preferred_element_type=F32)
    return d(0, 0) + d(1, 0) + d(2, 0) + d(0, 1) + d(1, 1) + d(0, 2)


def table(i, values):
    out = values[0]
    for k, v in enumerate(values):
        if v != values[0]:
            out = jnp.where(i == k, v, out)
    return out


def kernel(x_ref, l_ref, r_ref, w_ref, y_ref, xg, rx, ys, yr,
           t_ref, xbuf, lbuf, lsp, acc, rbuf, yrbuf,
           ssem, rsem, zsend, zrecv, bsend, brecv, ysend, yrecv, xsem, lsem, bsem, asem, ysem, osem):
    z = lax.axis_index('by')
    me = lax.axis_index('bx')
    core = lax.rem(me, 2)
    cx = lax.rem(me // 2, 2)
    cy = me // 4
    nf = x_ref.shape[3] // FB
    nb = x_ref.shape[3] // BT
    rows = x_ref.shape[0]
    half = rows // 2
    cols = x_ref.shape[3]

    def index(dx, dy, dc):
        return (lax.rem(cy + dy, 2) * 2 + lax.rem(cx + dx, 2)) * 2 + lax.rem(core + dc, 2)

    sib, xn, yn, dn = index(0, 0, 1), index(1, 0, 0), index(0, 1, 0), index(1, 1, 0)
    dev_s, dev_x, dev_y, dev_z = (z, sib), (z, xn), (z, yn), (1 - z, me)

    barrier = pltpu.get_barrier_semaphore()
    for dev in (dev_s, dev_x, dev_y, dev_z):
        pl.semaphore_signal(barrier, inc=1, device_id=dev, device_id_type=MESH)
    pl.semaphore_wait(barrier, 4)

    def piece(ref, k):
        return ref.at[:, :, :, pl.ds(pl.multiple_of(k * FB, FB), FB)]

    def rcopy(src, dst, kind, k, dev):
        return pltpu.make_async_remote_copy(src_ref=src, dst_ref=dst, send_sem=ssem.at[kind, k], recv_sem=rsem.at[kind, k],
                                            device_id=dev, device_id_type=MESH)

    def copy(kind, k):
        if kind == 0:
            return rcopy(piece(x_ref, k), piece(xg.at[me], k), 0, k, dev_s)
        if kind == 1:
            return rcopy(piece(x_ref, k), piece(xg.at[me], k), 1, k, dev_x)
        if kind == 2:
            return rcopy(piece(x_ref, k), piece(xg.at[me], k), 2, k, dev_y)
        if kind == 3:
            part = piece(xg.at[yn, pl.ds(0, half)], k)
            return rcopy(part, part, 3, k, dev_x)
        if kind == 4:
            part = piece(xg.at[xn, pl.ds(half, half)], k)
            return rcopy(part, part, 4, k, dev_y)
        part = piece(xg.at[(xn, yn, dn)[kind - 5]], k)
        return rcopy(part, part, kind, k, dev_s)

    def got(kind, k):
        if kind == 0:
            part = piece(xg.at[sib], k)
        elif kind == 1:
            part = piece(xg.at[xn], k)
        elif kind == 2:
            part = piece(xg.at[yn], k)
        elif kind == 3:
            part = piece(xg.at[dn, pl.ds(0, half)], k)
        elif kind == 4:
            part = piece(xg.at[dn, pl.ds(half, half)], k)
        else:
            part = piece(xg.at[(index(1, 0, 1), index(0, 1, 1), index(1, 1, 1))[kind - 5]], k)
        return rcopy(part, part, kind, k, dev_s)

    hw = cols // 2

    def rz(bt):
        rws = pl.ds(bt * BT, BT)
        src = r_ref.at[:, rws, pl.ds(pl.multiple_of((1 - z) * cols + core * hw, 128), hw)]
        dst = rx.at[:, rws, pl.ds(pl.multiple_of(core * hw, 128), hw)]
        return pltpu.make_async_remote_copy(src_ref=src, dst_ref=dst, send_sem=zsend.at[bt], recv_sem=zrecv.at[bt],
                                            device_id=dev_z, device_id_type=MESH)

    def rs(bt, c):
        part = rx.at[:, pl.ds(bt * BT, BT), pl.ds(pl.multiple_of(c * hw, 128), hw)]
        return pltpu.make_async_remote_copy(src_ref=part, dst_ref=part, send_sem=bsend.at[bt], recv_sem=brecv.at[bt],
                                            device_id=dev_s, device_id_type=MESH)

    def yz(bt):
        return pltpu.make_async_remote_copy(src_ref=ys.at[bt], dst_ref=yr.at[bt], send_sem=ysend.at[bt], recv_sem=yrecv.at[bt],
                                            device_id=dev_z, device_id_type=MESH)

    def own_out(k):
        copy(1, k).start()
        copy(2, k).start()

    def event_xy(k):
        got(1, k).wait_recv()
        copy(4, k).start()
        copy(5, k).start()
        got(2, k).wait_recv()
        copy(3, k).start()
        copy(6, k).start()

    def event_d(k):
        got(3, k).wait_recv()
        got(4, k).wait_recv()
        copy(7, k).start()

    def event_r(bt):
        rz(bt).wait_recv()
        rs(bt, core).start()

    events = {i: [] for i in range(len(UNITS))}
    events[3] += [lambda: event_xy(0), lambda: own_out(2)]
    events[6] += [lambda: event_xy(1), lambda: own_out(3)]
    events[8] += [lambda: event_d(0)]
    for k in range(2, 6):
        i = UNITS.index((XN, k)) - 1
        events[i] += [functools.partial(event_xy, k)]
        if k + 2 < 6:
            events[i] += [functools.partial(own_out, k + 2)]
    for k in range(1, 6):
        i = UNITS.index((DN, k)) - 1
        events[i] += [functools.partial(event_d, k)]
    events[12] += [lambda: event_r(0)]
    events[19] += [lambda: event_r(1)]

    def xload(slot, rel, k):
        px = lax.rem(cx + lax.rem(rel, 2), 2)
        py = lax.rem(cy + rel // 2, 2)
        chip = py * 2 + px
        a = pltpu.make_async_copy(piece(xg.at[chip * 2 + core], k), xbuf.at[slot, core], xsem.at[slot, 0])
        o = pltpu.make_async_copy(piece(x_ref, k), xbuf.at[slot, core], xsem.at[slot, 0])
        b = pltpu.make_async_copy(piece(xg.at[chip * 2 + 1 - core], k), xbuf.at[slot, 1 - core], xsem.at[slot, 1])
        lc = pltpu.make_async_copy(l_ref.at[:, :, pl.ds(pl.multiple_of(chip * 2 * rows, 128), 2 * rows)], lbuf, lsem)
        return a, o, b, lc

    copy(0, 0).start()
    own_out(0)
    for bt in range(nb):
        rz(bt).start()
    own_out(1)
    for k in range(1, nf):
        copy(0, k).start()

    def zero(i, carry):
        for c in range(12):
            t_ref[i, c] = jnp.zeros(t_ref.shape[2:], F32)
        return carry
    lax.fori_loop(0, nf, zero, 0)

    got(0, 0).wait_recv()
    _, o, b, lc = xload(0, 0, 0)
    o.start()
    b.start()
    lc.start()

    def unit(i, carry):
        slot = lax.rem(i, 2)
        rel, k = table(i, [u[0] for u in UNITS]), table(i, [u[1] for u in UNITS])
        nrel, nk = table(i, [u[0] for u in UNITS[1:]] + [0]), table(i, [u[1] for u in UNITS[1:]] + [0])
        for j, acts in events.items():
            if acts:
                @pl.when(i == j)
                def _():
                    for act in acts:
                        act()
        a, o, b, lc = xload(slot, rel, k)
        a.wait()
        b.wait()
        lc.wait()
        for c3 in range(3):
            for u in range(3):
                cs = slice(c3 * 256, (c3 + 1) * 256)
                hi, mid, low = split3(lbuf[u, :, cs])
                lsp[0, u, :, cs] = hi
                lsp[1, u, :, cs] = mid
                lsp[2, u, :, cs] = low

        @pl.when(i + 1 < len(UNITS))
        def _():
            for n, kind in ((OWN, (0,)), (XN, (5,)), (YN, (6,)), (DN, (7,))):
                @pl.when(nrel == n)
                def _():
                    for kd in kind:
                        got(kd, nk).wait_recv()
            na, no, nbb, nl = xload(1 - slot, nrel, nk)

            @pl.when(nrel == OWN)
            def _():
                no.start()

            @pl.when(nrel != OWN)
            def _():
                na.start()
            nbb.start()
            nl.start()
        for p in range(2):
            for q in range(2):
                xs = jnp.concatenate([xbuf[slot, 0, :, p, q, :], xbuf[slot, 1, :, p, q, :]], axis=0)
                xparts = split3(xs)
                for u in range(3):
                    idx = (u * 2 + p) * 2 + q
                    t_ref[k, idx] = dot6([lsp[j, u] for j in range(3)], xparts, 0) + t_ref[k, idx]

        @pl.when(rel == DN)
        def _():
            mix(k)
        return carry

    def mix(k):
        w = [w_ref[j] for j in range(36)]

        def wt(u, s, p, v):
            return w[((u * 2 + s) * 2 + p) * 3 + v]

        def rows8(j, carry):
            for h in range(FB // 128):
                sl = (pl.ds(pl.multiple_of(j * 8, 8), 8), slice(h * 128, (h + 1) * 128))
                t = [t_ref[(k, c) + sl] for c in range(12)]
                md = {}
                for s in range(2):
                    for v in range(3):
                        for q in range(2):
                            terms = [t[(u * 2 + p) * 2 + q] * wt(u, s, p, v) for u in range(3) for p in range(2)]
                            md[s, v, q] = functools.reduce(lambda m, n: m + n, terms)
                for s in range(2):
                    for tt in range(2):
                        for r in range(3):
                            terms = [md[s, v, q] * wt(v, tt, q, r) for v in range(3) for q in range(2)]
                            t_ref[(k, (s * 2 + tt) * 3 + r) + sl] = functools.reduce(lambda m, n: m + n, terms)
            return carry
        lax.fori_loop(0, rows // 8, rows8, 0)

    lax.fori_loop(0, len(UNITS), unit, 0)

    ntile = 2 * nb
    nunit = ntile * nf

    def rload(slot, j):
        tile = j // nf
        k = lax.rem(j, nf)
        bt = lax.rem(tile, nb)
        rws = pl.ds(pl.multiple_of(bt * BT, BT), BT)
        other = pltpu.make_async_copy(rx.at[:, rws, pl.ds(pl.multiple_of(k * FB, FB), FB)], rbuf.at[slot], bsem.at[slot])
        own = pltpu.make_async_copy(r_ref.at[:, rws, pl.ds(pl.multiple_of(z * cols + k * FB, FB), FB)], rbuf.at[slot],
                                    bsem.at[slot])
        return other, own

    rs(0, 1 - core).wait_recv()
    rload(0, 0)[0].start()
    event_r(2)

    def aflush(slot, bt):
        return pltpu.make_async_copy(acc.at[slot], ys.at[bt], asem)

    def yout(bt, h):
        return pltpu.make_async_copy(xbuf.at[0, h], y_ref.at[:, :, :, pl.ds(pl.multiple_of(bt * BT + h * FB, FB), FB)],
                                     osem.at[h])

    def yload(bt):
        return pltpu.make_async_copy(yr.at[bt], yrbuf, ysem)

    def unit2(j, carry):
        slot = lax.rem(j, 2)
        tile = j // nf
        k = lax.rem(j, nf)
        bt = lax.rem(tile, nb)
        aslot = lax.rem(tile, 2)

        @pl.when(k == 0)
        def _():
            for st in range(4):
                acc[aslot, st] = jnp.zeros(acc.shape[2:], F32)
        rload(slot, j)[0].wait()
        for bt_ in range(1, nb):
            @pl.when(j + 1 == bt_ * nf)
            def _():
                rs(bt_, 1 - core).wait_recv()

        @pl.when(j + 1 < nb * nf)
        def _():
            rload(1 - slot, j + 1)[0].start()

        @pl.when(jnp.logical_and(j + 1 >= nb * nf, j + 1 < nunit))
        def _():
            rload(1 - slot, j + 1)[1].start()

        @pl.when(jnp.logical_and(tile >= nb, k == nf - 1))
        def _():
            yz(bt).wait_recv()
            yload(bt).start()
        rparts = [split3(rbuf[slot, r]) for r in range(3)]
        for st in range(4):
            tot = acc[aslot, st]
            for r in range(3):
                tot = dot6(split3(t_ref[k, st * 3 + r]), rparts[r], 1) + tot
            acc[aslot, st] = tot

        @pl.when(jnp.logical_and(jnp.logical_and(tile >= 1, tile <= nb), k == 0))
        def _():
            aflush(1 - aslot, tile - 1).wait()
            yz(tile - 1).start()

        @pl.when(jnp.logical_and(tile < nb, k == nf - 1))
        def _():
            aflush(aslot, bt).start()

        @pl.when(jnp.logical_and(tile >= nb, k == nf - 1))
        def _():
            yload(bt).wait()

            @pl.when(tile > nb)
            def _():
                for h in range(2):
                    yout(bt - 1, h).wait()
            for s in range(2):
                for tt in range(2):
                    for h in range(2):
                        cs = slice(h * FB, (h + 1) * FB)
                        xbuf[0, h, :, s, tt, :] = acc[aslot, s * 2 + tt, :, cs] + yrbuf[s * 2 + tt, :, cs]
            for h in range(2):
                yout(bt, h).start()
        return carry

    lax.fori_loop(0, nunit, unit2, 0)
    for h in range(2):
        yout(nb - 1, h).wait()
    for bt in range(nb):
        rz(bt).wait_send()
        rs(bt, core).wait_send()
        yz(bt).wait_send()
    for k in range(nf):
        for kind in range(8):
            copy(kind, k).wait_send()


def apply_local(x, left, w, right):
    rows, cols = x.shape[0], x.shape[3]
    lt = jnp.transpose(left, (1, 0, 2))
    rt = jnp.transpose(right, (1, 0, 2))
    nf, nb = cols // FB, cols // BT
    hbm = pl.BlockSpec(memory_space=pltpu.HBM)
    S = jax.ShapeDtypeStruct
    dma = pltpu.SemaphoreType.DMA
    out = pl.pallas_call(
        kernel,
        out_shape=[S(x.shape, F32), S((8,) + x.shape, F32), S((3, cols, cols), F32), S((nb, 4, rows, BT), F32),
                   S((nb, 4, rows, BT), F32)],
        in_specs=[hbm, hbm, hbm, pl.BlockSpec(memory_space=pltpu.SMEM)],
        out_specs=[hbm] * 5,
        scratch_shapes=[
            pltpu.VMEM((nf, 12, rows, FB), F32),
            pltpu.VMEM((2, 2, rows, 2, 2, FB), F32),
            pltpu.VMEM((3, rows, 2 * rows), F32),
            pltpu.VMEM((3, 3, rows, 2 * rows), BF),
            pltpu.VMEM((2, 4, rows, BT), F32),
            pltpu.VMEM((2, 3, BT, FB), F32),
            pltpu.VMEM((4, rows, BT), F32),
            dma((8, nf)), dma((8, nf)), dma((nb,)), dma((nb,)), dma((nb,)), dma((nb,)), dma((nb,)), dma((nb,)),
            dma((2, 2)), dma, dma((2,)), dma, dma, dma((2,)),
        ],
        compiler_params=pltpu.CompilerParams(collective_id=0, has_side_effects=True, vmem_limit_bytes=67043328),
        name="heff",
    )(x, lt, rt, w.reshape(36))
    return out[0]


def solution(mesh):
    return jax.shard_map(apply_local, mesh=mesh,
                         in_specs=(P('bx', None, None, 'by'), P('bx', None, None), P(), P('by', None, None)),
                         out_specs=P('bx', None, None, 'by'), check_vma=False)
```

time: 2200 us -> 647 us (0.29)
  waiting for transfers between devices: 1020 us -> 0 us
  matrix products: 767 us -> 0 us
  Pallas kernels: 0 us -> 635 us
  local copies, waits for them, and re-layouts: 360 us -> 9.83 us
  starting transfers between devices: 26.6 us -> 0 us
    all_to_all x1 -> x0, waiting for transfers between devices: 812 us -> none  [local_apply(): right_cols = lax.all_to_all(right_rows, 'by', 2, 0, tiled=True)]
    dot_general x4 -> x0, matrix products: 767 us -> none  [the longest x1 283 us: local_apply(): jnp.dot(left_rows.reshape(row_share * mpo_dim, bond_dim), wave_cols.resha...]
    pallas_call x0 -> x1, Pallas kernels: none -> 635 us  [apply_local(): pl.pallas_call(kernel, out_shape=[S(x.shape, F32), S((8,) + x.shape, F32)...]
    reduce_scatter x1 -> x0, waiting for transfers between devices: 210 us -> none  [local_apply(): return lax.psum_scatter(part_sum, 'by', scatter_dimension=3, tiled=True)]
    unnamed x6 -> x1, local copies, waits for them, and re-layouts: 118 us -> 8.54 us
    reshape x1, local copies, waits for them, and re-layouts: 108 us -> 1.29 us  [apply_local(): w.reshape(36)]
    all_to_all x1 -> x0, local copies, waits for them, and re-layouts: 78 us -> none  [local_apply(): right_cols = lax.all_to_all(right_rows, 'by', 2, 0, tiled=True)]
    transpose x1 -> x0, local copies, waits for them, and re-layouts: 38.9 us -> none  [local_apply(): jnp.einsum('asvqf,vtqr->astrf', stage_two, mpo_ten, precision=prec_mode,...]
  transfers between devices with their start and end apart: 3 -> 0, of which waited for: 2 -> 0; matrix products, arithmetic and copies ran while one was open for 9% -> 0% of each run, Pallas kernels for 0% -> 0%
where the time goes in v1:
time: 647 us; the launch traced here: 645 us
  Pallas kernels  635 us (98%)
  local copies, waits for them, and re-layouts  9.83 us (2%)
    pallas_call x1, Pallas kernels, apply_local(): pl.pallas_call(kernel, out_shape=[S(x.shape, F32), S((8,) + x.shape, F32)...  635 us

profile of v1, /device:TPU:0, one launch (start us, length us, event | category | flops | bytes accessed | tf_op | source)
XLA Modules:
  0.0 645.2 jit_solution(3003809663123322579)
XLA Ops:
  0.0 1.3 reshape.3.w_ref
  1.3 635.3 %heff.1 = (f32[384,2,2,1536]{3,2,1,0:T(2,128)}, f32[8,384,2,2,1536]{4,3,2,1,0:T(2,128)}, f32[3,1536,1536]{2,1,0:T(8,128)}, f32[3,4,384,512]{3,2,1,0:T(8,128)}, f32[3,4,384,512]{3,2,1,0:T(8,128)}) custom-call(f32[384,2,2,1536]{3,2,1,0:T(2,128)} %x_ref.1, f32[3,384,3072]{2,1,0:T(8,128)} %bitcast.3, f32[3,1536,3072]{2,1,0:T(8,128)} %bitcast.2, f32[36]{0:T(128)} %reshape.3.w_ref), custom_call_target="tpu_custom_call" | custom-call | tf_op jit(solution)/shard_map/heff/pallas_call | solution.py:379
  636.6 8.5 %copy.6 = f32[384,2,2,1536]{3,2,1,0:T(2,128)} copy(f32[384,2,2,1536]{3,2,1,0:T(2,128)} %get-tuple-element.6) | data formatting | bytes 18874368

commit v2 on v0

v2 whole, which is shorter than its diff:
```python
import functools
import jax
import jax.numpy as jnp
from jax import lax
from jax.experimental import pallas as pl
from jax.experimental.pallas import tpu as pltpu
from jax.sharding import PartitionSpec as P

MESH = pl.DeviceIdType.MESH
BF, F32 = jnp.bfloat16, jnp.float32
FB = 256
BT = 512

OWN, XN, YN, DN = 0, 1, 2, 3


def S(rel, k):
    return ('s', rel, k)


def Q(own, bt, pair):
    return ('t', own, bt, pair)


UNITS = [S(OWN, 0), S(OWN, 1), S(OWN, 2), S(OWN, 3), S(OWN, 4), S(XN, 0), S(YN, 0), S(OWN, 5), S(XN, 1), S(DN, 0), S(YN, 1)]
UNITS += [S(XN, 2), S(YN, 2), S(DN, 1), Q(0, 0, 0), S(XN, 3), S(YN, 3), S(DN, 2), Q(0, 1, 0), S(XN, 4), S(YN, 4), S(DN, 3)]
UNITS += [Q(0, 0, 1), S(XN, 5), S(YN, 5), S(DN, 4), S(DN, 5), Q(0, 0, 2)]
UNITS += [Q(0, 1, 1), Q(0, 1, 2)] + [Q(0, 2, pair) for pair in range(3)]
UNITS += [Q(1, bt, pair) for bt in range(3) for pair in range(3)]
MIX_AFTER = {S(DN, k): k for k in range(6)}
LATE = {S(XN, 5), S(DN, 5)}
AT = {
    S(OWN, 3): ['xy0', 'own2'], S(YN, 0): ['xy1', 'own3'], S(OWN, 5): ['d0'], S(YN, 1): ['r0'],
    S(XN, 2): ['d1'], S(XN, 3): ['d2'], S(YN, 3): ['r1'], S(XN, 4): ['d3'], Q(0, 0, 1): ['xy5'], S(XN, 5): ['d4'],
    S(DN, 4): ['d5'], S(DN, 5): ['r2'],
}
MID = {
    S(DN, 0): ['xy2', 'own4'], S(DN, 1): ['xy3', 'own5'], S(DN, 2): ['xy4'],
}


def split3(v):
    hi = v.astype(BF)
    rest = v - hi.astype(F32)
    mid = rest.astype(BF)
    low = (rest - mid.astype(F32)).astype(BF)
    return hi, mid, low


def dot6(a, b, rhs_dim):
    def d(i, j):
        return lax.dot_general(a[i], b[j], (((1,), (rhs_dim,)), ((), ())), preferred_element_type=F32)
    return d(0, 0) + d(1, 0) + d(2, 0) + d(0, 1) + d(1, 1) + d(0, 2)


def table(i, values):
    out = values[0]
    for k, v in enumerate(values):
        if v != values[0]:
            out = jnp.where(i == k, v, out)
    return out


def kernel(x_ref, l_ref, r_ref, w_ref, y_ref, xg, rx, ys, yr, lc_ref,
           t_ref, xbuf, lsp, acc, rbuf,
           ssem, rsem, zsend, zrecv, bsend, brecv, ysend, yrecv, xsem, lsem, csem, psem, bsem, asem, ysem, osem):
    z = lax.axis_index('by')
    me = lax.axis_index('bx')
    core = lax.rem(me, 2)
    cx = lax.rem(me // 2, 2)
    cy = me // 4
    rows, cols = x_ref.shape[0], x_ref.shape[3]
    nf, nb = cols // FB, cols // BT
    half = rows // 2
    hw = cols // 2

    def index(dx, dy, dc):
        return (lax.rem(cy + dy, 2) * 2 + lax.rem(cx + dx, 2)) * 2 + lax.rem(core + dc, 2)

    sib, xn, yn, dn = index(0, 0, 1), index(1, 0, 0), index(0, 1, 0), index(1, 1, 0)
    dev_s, dev_x, dev_y, dev_z = (z, sib), (z, xn), (z, yn), (1 - z, me)

    barrier = pltpu.get_barrier_semaphore()
    for dev in (dev_s, dev_x, dev_y, dev_z):
        pl.semaphore_signal(barrier, inc=1, device_id=dev, device_id_type=MESH)
    pl.semaphore_wait(barrier, 4)

    def remote(src, dst, send, recv, dev):
        return pltpu.make_async_remote_copy(src_ref=src, dst_ref=dst, send_sem=send, recv_sem=recv, device_id=dev,
                                            device_id_type=MESH)

    def piece(ref, k):
        return ref.at[:, :, :, pl.ds(pl.multiple_of(k * FB, FB), FB)]

    def block(kind):
        if kind < 3:
            return xg.at[me]
        if kind == 3:
            return xg.at[yn, pl.ds(0, half)]
        if kind == 4:
            return xg.at[xn, pl.ds(half, half)]
        return xg.at[(xn, yn, dn)[kind - 5]]

    def send(kind, k):
        dst = piece(block(kind), k) if kind or k > 1 else xbuf.at[k, core]
        src = piece(x_ref, k) if kind < 3 else dst
        dev = (dev_s, dev_x, dev_y, dev_x, dev_y, dev_s, dev_s, dev_s)[kind]
        return remote(src, dst, ssem.at[kind, k], rsem.at[kind, k], dev)

    def arrived(kind, k):
        ref = (xg.at[sib], xg.at[xn], xg.at[yn], xg.at[dn, pl.ds(0, half)], xg.at[dn, pl.ds(half, half)],
               xg.at[index(1, 0, 1)], xg.at[index(0, 1, 1)], xg.at[index(1, 1, 1)])[kind]
        part = piece(ref, k) if kind or not isinstance(k, int) else xbuf.at[k, 1 - core]
        remote(part, part, ssem.at[kind, k], rsem.at[kind, k], dev_s).wait_recv()

    def rz(bt):
        rws = pl.ds(bt * BT, BT)
        src = r_ref.at[:, rws, pl.ds(pl.multiple_of((1 - z) * cols + core * hw, 128), hw)]
        dst = rx.at[:, rws, pl.ds(pl.multiple_of(core * hw, 128), hw)]
        return remote(src, dst, zsend.at[bt], zrecv.at[bt], dev_z)

    def rs(bt, c):
        part = rx.at[:, pl.ds(pl.multiple_of(bt * BT, BT), BT), pl.ds(pl.multiple_of(c * hw, 128), hw)]
        return remote(part, part, bsend.at[bt], brecv.at[bt], dev_s)

    def yz(bt):
        return remote(ys.at[bt], yr.at[bt], ysend.at[bt], yrecv.at[bt], dev_z)

    def run(name):
        k = int(name[-1])
        if name[:-1] == 'own':
            send(1, k).start()
            send(2, k).start()
        elif name[:-1] == 'xy':
            arrived(1, k)
            send(4, k).start()
            send(5, k).start()
            arrived(2, k)
            send(3, k).start()
            send(6, k).start()
        elif name[:-1] == 'd':
            arrived(3, k)
            arrived(4, k)
            send(7, k).start()
        elif name[:-1] == 'r':
            rz(k).wait_recv()
            rs(k, core).start()
        elif name[:-1] == 'f':
            flush(0, k).wait()
            yz(k).start()
        elif name[:-1] == 'y':
            yz(k).wait_recv()
            yload(yslot[k], k).start()

    n = len(UNITS)
    xslot, lslot, lmode, rslot = [0] * n, [0] * n, [0] * n, [0] * n
    cnt, prev, ls, seen, rcnt = 0, None, 1, set(), 0
    writes = {}
    for i, u in enumerate(UNITS):
        if u[0] == 's':
            xslot[i] = cnt % 2
            cnt += 1
            if u[1] != prev:
                ls = 1 - ls
                lmode[i] = 2 if u[1] in seen else 1
                if lmode[i] == 1:
                    nxt = next(j for j in range(i + 1, n) if UNITS[j][0] == 's')
                    writes[nxt] = u[1]
                seen.add(u[1])
                prev = u[1]
            lslot[i] = ls
        else:
            rslot[i] = rcnt % 2
            rcnt += 1
    lmode[0] = 0
    at = {i: list(AT.get(u, ())) for i, u in enumerate(UNITS)}
    mid = {i: list(MID.get(u, ())) for i, u in enumerate(UNITS)}
    mixk = [0 for u in UNITS]
    mixa = [MIX_AFTER.get(u, -1) + 1 for u in UNITS]
    init = [int(u[0] == 's' and all(v[0] != 's' or v[2] != u[2] for v in UNITS[:i])) for i, u in enumerate(UNITS)]
    sums = [i for i, u in enumerate(UNITS) if u[0] == 't']
    aslot, first, last = [0] * n, [0] * n, [0] * n
    order, yslot = [], {}
    for i in sums:
        tile = UNITS[i][1:3]
        if tile not in order:
            order.append(tile)
            first[i] = 1
        aslot[i] = order.index(tile) % 2
        yslot[tile[1]] = 1 - aslot[i]
        if all(UNITS[j][1:3] != tile for j in sums if j > i):
            last[i] = 1
            if tile[0] == 0:
                at[i + (1 if tile[1] == 0 else 2)].append('f%d' % tile[1])
            else:
                if tile[1] < nb - 1:
                    at[i].append('y%d' % tile[1])
    is_t = [int(u[0] == 't') for u in UNITS]
    arg = [[u[j] if len(u) > j else 0 for u in UNITS] for j in range(1, 4)]
    late = [int(u in LATE) for u in UNITS]

    def chip(rel):
        return lax.rem(cy + rel // 2, 2) * 2 + lax.rem(cx + lax.rem(rel, 2), 2)

    def xcopies(slot, rel, k):
        c = chip(rel) * 2
        return (pltpu.make_async_copy(piece(x_ref, k), xbuf.at[slot, core], xsem.at[slot, 0]),
                pltpu.make_async_copy(piece(xg.at[c + core], k), xbuf.at[slot, core], xsem.at[slot, 0]),
                pltpu.make_async_copy(piece(xg.at[c + 1 - core], k), xbuf.at[slot, 1 - core], xsem.at[slot, 1]))

    def xstart(slot, rel, k):
        own, far, sibling = xcopies(slot, rel, k)

        @pl.when(rel == OWN)
        def _():
            own.start()

        @pl.when(rel != OWN)
        def _():
            far.start()
        for r, kind in ((OWN, 0), (XN, 5), (YN, 6), (DN, 7)):
            @pl.when(rel == r)
            def _():
                arrived(kind, k)
        sibling.start()

    def lcopies(rel, what):
        base = chip(rel) * 2 * rows
        for j, (dst, off, width) in enumerate(((acc.at[0, pl.ds(0, 3)], 0, BT), (acc.at[1, pl.ds(0, 3), :, pl.ds(0, FB)], BT, FB))):
            src = l_ref.at[:, :, pl.ds(pl.multiple_of(base + off, 128), width)]
            getattr(pltpu.make_async_copy(src, dst, lsem.at[j]), what)()

    def cload(slot, rel):
        return pltpu.make_async_copy(lc_ref.at[rel], lsp.at[slot], csem)

    def cstore(slot, rel):
        return pltpu.make_async_copy(lsp.at[slot], lc_ref.at[rel], psem)

    def rcopies(slot, bt, pair):
        rws = pl.ds(pl.multiple_of(bt * BT, BT), BT)
        return (pltpu.make_async_copy(rx.at[:, rws, pl.ds(pl.multiple_of(pair * 512, 512), 512)], rbuf.at[slot], bsem.at[slot]),
                pltpu.make_async_copy(r_ref.at[:, rws, pl.ds(pl.multiple_of(z * cols + pair * 512, 512), 512)], rbuf.at[slot],
                                      bsem.at[slot]))

    def flush(slot, bt):
        return pltpu.make_async_copy(acc.at[slot], ys.at[bt], asem)

    def yload(slot, bt):
        return pltpu.make_async_copy(yr.at[bt], acc.at[slot], ysem)

    def yout(bt, h):
        return pltpu.make_async_copy(xbuf.at[1, h], y_ref.at[:, :, :, pl.ds(pl.multiple_of(bt * BT + h * FB, FB), FB)],
                                     osem.at[h])

    def lsplit(slot):
        def body(j, carry):
            sl = pl.ds(pl.multiple_of(j * 16, 16), 16)
            for u in range(3):
                for j, (off, width) in enumerate(((0, BT), (BT, FB))):
                    for part, v in enumerate(split3(acc[j, u, sl, :width])):
                        lsp[slot, part, u, sl, off:off + width] = v
            return carry
        lax.fori_loop(0, rows // 16, body, 0, unroll=2)

    for k in range(2):
        send(0, k).start()
    lcopies(OWN, 'start')
    for k in range(2):
        xcopies(k, OWN, k)[0].start()
    run('own0')
    for bt in range(nb):
        rz(bt).start()
    run('own1')
    for k in range(2, nf):
        send(0, k).start()
    lcopies(OWN, 'wait')
    lsplit(0)
    cstore(0, OWN).start()
    xcopies(0, OWN, 0)[0].wait()
    arrived(0, 0)

    def mix8(k, row):
        w = {(u, s, p, v): w_ref[u, s, p, v] for u in range(3) for s in range(2) for p in range(2) for v in range(3)}

        def wt(u, s, p, v):
            return w[u, s, p, v]

        for h in range(FB // 128):
            sl = (pl.ds(pl.multiple_of(row, 8), 8), slice(h * 128, (h + 1) * 128))
            t = [t_ref[(k, c) + sl] for c in range(12)]
            md = {}
            for s in range(2):
                for v in range(3):
                    for q in range(2):
                        terms = [t[(u * 2 + p) * 2 + q] * wt(u, s, p, v) for u in range(3) for p in range(2)]
                        md[s, v, q] = functools.reduce(lambda m, o: m + o, terms)
            for s in range(2):
                for tt in range(2):
                    for r in range(3):
                        terms = [md[s, v, q] * wt(v, tt, q, r) for v in range(3) for q in range(2)]
                        t_ref[(k, (s * 2 + tt) * 3 + r) + sl] = functools.reduce(lambda m, o: m + o, terms)

    writes = set(writes)
    fields = [(is_t, 2), (arg[0], 4), (arg[1], 8), (arg[2], 4), (xslot, 2), (lslot, 2), (lmode, 4), (rslot, 2), (aslot, 2),
              (first, 2), (last, 2), (late, 2), ([int(bool(at[i]) or i in writes) for i in range(n)], 2),
              ([int(bool(mid[i])) for i in range(n)], 2), (mixk, 8), (mixa, 8), (init, 2)]
    codes = []
    for i in range(n):
        code = 0
        for values, base in reversed(fields):
            code = code * base + values[i]
        codes.append(code)

    def decode(code):
        out = []
        for _, base in fields:
            out.append(jnp.bitwise_and(code, base - 1))
            code = jnp.right_shift(code, base.bit_length() - 1)
        return out

    def unit(i, code):
        kind, a0, a1, a2, xs_, ls_, lm_, rs_, as_, first_, last_, late_, ev_, evm_, mixk_, mixa_, init_ = decode(code)
        code1 = table(i, codes[1:] + [0])
        kind1, b0, b1, b2, xs1, ls1, lm1, rs1, _, first1, _, late1 = decode(code1)[:12]

        @pl.when(ev_ == 1)
        def _():
            for j in range(n):
                if at[j] or j in writes:
                    @pl.when(i == j)
                    def _():
                        if j in writes:
                            cstore(0, 0).wait()
                        for name in at[j]:
                            run(name)

        @pl.when(kind == 0)
        def _():
            @pl.when(late_ == 1)
            def _():
                xstart(xs_, a0, a1)
            @pl.when(i == 1)
            def _():
                xcopies(1, OWN, 1)[0].wait()
                arrived(0, 1)

            @pl.when(i > 1)
            def _():
                _, far, sibling = xcopies(xs_, a0, a1)
                far.wait()
                sibling.wait()

            @pl.when(lm_ == 1)
            def _():
                lcopies(a0, 'wait')
                lsplit(ls_)
                cstore(ls_, a0).start()

            @pl.when(lm_ == 2)
            def _():
                cload(ls_, a0).wait()

        @pl.when(kind == 1)
        def _():
            rcopies(rs_, a1, a2)[0].wait()

        def ahead():
            @pl.when(kind1 == 0)
            def _():
                @pl.when(jnp.logical_and(late1 == 0, i > 0))
                def _():
                    xstart(xs1, b0, b1)

                @pl.when(lm1 == 1)
                def _():
                    lcopies(b0, 'start')

                @pl.when(lm1 == 2)
                def _():
                    cload(ls1, b0).start()

            @pl.when(kind1 == 1)
            def _():
                @pl.when(b0 == 0)
                def _():
                    @pl.when(first1 == 1)
                    def _():
                        rs(b1, 1 - core).wait_recv()
                    rcopies(rs1, b1, b2)[0].start()

                @pl.when(b0 == 1)
                def _():
                    rcopies(rs1, b1, b2)[1].start()

        @pl.when(i + 1 < n)
        def _():
            ahead()

        @pl.when(kind == 0)
        def _():
            for p in range(2):
                for q in range(2):
                    xs = jnp.concatenate([xbuf[xs_, 0, :, p, q, :], xbuf[xs_, 1, :, p, q, :]], axis=0)
                    xparts = split3(xs)
                    for u in range(3):
                        idx = (u * 2 + p) * 2 + q
                        old = jnp.where(init_ == 1, 0.0, t_ref[a1, idx])
                        t_ref[a1, idx] = dot6([lsp[ls_, j, u] for j in range(3)], xparts, 0) + old

        @pl.when(evm_ == 1)
        def _():
            for j in range(n):
                if mid[j]:
                    @pl.when(i == j)
                    def _():
                        for name in mid[j]:
                            run(name)

        @pl.when(mixa_ > 0)
        def _():
            def body(j, carry):
                mix8(mixa_ - 1, j * 8)
                return carry
            lax.fori_loop(0, rows // 8, body, 0, unroll=4)

        @pl.when(kind == 1)
        def _():
            rparts = [[split3(rbuf[rs_, r, :, f * FB:(f + 1) * FB]) for f in range(2)] for r in range(3)]
            for st in range(4):
                tot = jnp.where(first_ == 1, 0.0, acc[as_, st])
                for r in range(3):
                    for f in range(2):
                        tot = dot6(split3(t_ref[a2 * 2 + f, st * 3 + r]), rparts[r][f], 1) + tot
                acc[as_, st] = tot

            @pl.when(last_ == 1)
            def _():
                @pl.when(a0 == 0)
                def _():
                    flush(as_, a1).start()

                @pl.when(a0 == 1)
                def _():
                    @pl.when(i == n - 1)
                    def _():
                        run('y%d' % (nb - 1))

                    @pl.when(a1 > 0)
                    def _():
                        for h in range(2):
                            yout(a1 - 1, h).wait()
                    yload(1 - as_, a1).wait()
                    for h in range(2):
                        for s in range(2):
                            for tt in range(2):
                                st = s * 2 + tt
                                part = acc[1 - as_, st, :, h * FB:(h + 1) * FB]
                                xbuf[1, h, :, s, tt, :] = acc[as_, st, :, h * FB:(h + 1) * FB] + part
                        yout(a1, h).start()
        return code1

    lax.fori_loop(0, n, unit, jnp.int32(codes[0]))
    for h in range(2):
        yout(nb - 1, h).wait()
    for bt in range(nb):
        rz(bt).wait_send()
        rs(bt, core).wait_send()
        yz(bt).wait_send()
    for k in range(nf):
        for kd in range(8):
            send(kd, k).wait_send()


def apply_local(x, left, w, right):
    rows, cols = x.shape[0], x.shape[3]
    lt = jnp.transpose(left, (1, 0, 2))
    rt = jnp.transpose(right, (1, 0, 2))
    nf, nb = cols // FB, cols // BT
    hbm = pl.BlockSpec(memory_space=pltpu.HBM)
    shape = jax.ShapeDtypeStruct
    dma = pltpu.SemaphoreType.DMA
    tiles = shape((nb, 4, rows, BT), F32)
    out = pl.pallas_call(
        kernel,
        out_shape=[shape(x.shape, F32), shape((8,) + x.shape, F32), shape((3, cols, cols), F32), tiles, tiles,
                   shape((4, 3, 3, rows, 2 * rows), BF)],
        in_specs=[hbm, hbm, hbm, pl.BlockSpec(memory_space=pltpu.SMEM)],
        out_specs=[hbm] * 6,
        scratch_shapes=[
            pltpu.VMEM((nf, 12, rows, FB), F32),
            pltpu.VMEM((2, 2, rows, 2, 2, FB), F32),
            pltpu.VMEM((2, 3, 3, rows, 2 * rows), BF),
            pltpu.VMEM((2, 4, rows, BT), F32),
            pltpu.VMEM((2, 3, BT, 512), F32),
            dma((8, nf)), dma((8, nf)), dma((nb,)), dma((nb,)), dma((nb,)), dma((nb,)), dma((nb,)), dma((nb,)),
            dma((2, 2)), dma((2,)), dma, dma, dma((2,)), dma, dma, dma((2,)),
        ],
        compiler_params=pltpu.CompilerParams(collective_id=0, has_side_effects=True, vmem_limit_bytes=67043328),
        name="heff",
    )(x, lt, rt, w)
    return out[0]


def solution(mesh):
    return jax.shard_map(apply_local, mesh=mesh,
                         in_specs=(P('bx', None, None, 'by'), P('bx', None, None), P(), P('by', None, None)),
                         out_specs=P('bx', None, None, 'by'), check_vma=False)
```

time: 2200 us -> 604 us (0.27)
  waiting for transfers between devices: 1020 us -> 0 us
  matrix products: 767 us -> 0 us
  Pallas kernels: 0 us -> 595 us
  local copies, waits for them, and re-layouts: 360 us -> 8.54 us
  starting transfers between devices: 26.6 us -> 0 us
    all_to_all x1 -> x0, waiting for transfers between devices: 812 us -> none  [local_apply(): right_cols = lax.all_to_all(right_rows, 'by', 2, 0, tiled=True)]
    dot_general x4 -> x0, matrix products: 767 us -> none  [the longest x1 283 us: local_apply(): jnp.dot(left_rows.reshape(row_share * mpo_dim, bond_dim), wave_cols.resha...]
    pallas_call x0 -> x1, Pallas kernels: none -> 595 us  [apply_local(): pl.pallas_call(kernel, out_shape=[shape(x.shape, F32), shape((8,) + x.sha...]
    reduce_scatter x1 -> x0, waiting for transfers between devices: 210 us -> none  [local_apply(): return lax.psum_scatter(part_sum, 'by', scatter_dimension=3, tiled=True)]
    unnamed x6 -> x1, local copies, waits for them, and re-layouts: 118 us -> 8.54 us
    reshape x1 -> x0, local copies, waits for them, and re-layouts: 108 us -> none  [local_apply(): wave_cols.reshape(bond_dim, phys_dim * phys_dim * col_share)]
    all_to_all x1 -> x0, local copies, waits for them, and re-layouts: 78 us -> none  [local_apply(): right_cols = lax.all_to_all(right_rows, 'by', 2, 0, tiled=True)]
    transpose x1 -> x0, local copies, waits for them, and re-layouts: 38.9 us -> none  [local_apply(): jnp.einsum('asvqf,vtqr->astrf', stage_two, mpo_ten, precision=prec_mode,...]
  transfers between devices with their start and end apart: 3 -> 0, of which waited for: 2 -> 0; matrix products, arithmetic and copies ran while one was open for 9% -> 0% of each run, Pallas kernels for 0% -> 0%
where the time goes in v2:
time: 604 us
  Pallas kernels  595 us (99%)
  local copies, waits for them, and re-layouts  8.54 us (1%)
    pallas_call x1, Pallas kernels, apply_local(): pl.pallas_call(kernel, out_shape=[shape(x.shape, F32), shape((8,) + x.sha...  595 us

profile of v2, /device:TPU:0, one launch (start us, length us, event | category | flops | bytes accessed | tf_op | source)
XLA Modules:
  0.0 603.7 jit_solution(8750753422642601033)
XLA Ops:
  0.0 595.1 %heff.1 = (f32[384,2,2,1536]{3,2,1,0:T(2,128)}, f32[8,384,2,2,1536]{4,3,2,1,0:T(2,128)}, f32[3,1536,1536]{2,1,0:T(8,128)}, f32[3,4,384,512]{3,2,1,0:T(8,128)}, f...) custom-call(f32[384,2,2,1536]{3,2,1,0:T(2,128)} %x_ref.1, f32[3,384,3072]{2,1,0:T(8,128)} %bitcast.3, ...), custom_call_target="tpu_custom_call" | custom-call | tf_op jit(solution)/shard_map/heff/pallas_call | solution.py:483
  595.1 8.5 %copy.6 = f32[384,2,2,1536]{3,2,1,0:T(2,128)} copy(f32[384,2,2,1536]{3,2,1,0:T(2,128)} %get-tuple-element.6) | data formatting | bytes 18874368

commit v3 on v2

--- a/solution.py
+++ b/solution.py
@@ -28,14 +28,15 @@
 UNITS += [Q(0, 1, 1), Q(0, 1, 2)] + [Q(0, 2, pair) for pair in range(3)]
 UNITS += [Q(1, bt, pair) for bt in range(3) for pair in range(3)]
 MIX_AFTER = {S(DN, k): k for k in range(6)}
-LATE = {S(XN, 5), S(DN, 5)}
+LATE = {S(DN, 5)}
 AT = {
     S(OWN, 3): ['xy0', 'own2'], S(YN, 0): ['xy1', 'own3'], S(OWN, 5): ['d0'], S(YN, 1): ['r0'],
-    S(XN, 2): ['d1'], S(XN, 3): ['d2'], S(YN, 3): ['r1'], S(XN, 4): ['d3'], Q(0, 0, 1): ['xy5'], S(XN, 5): ['d4'],
+    S(XN, 2): ['d1'], S(XN, 3): ['d2'], S(YN, 3): ['r1'], S(XN, 4): ['d3'], S(XN, 5): ['d4'],
     S(DN, 4): ['d5'], S(DN, 5): ['r2'],
 }
 MID = {
-    S(DN, 0): ['xy2', 'own4'], S(DN, 1): ['xy3', 'own5'], S(DN, 2): ['xy4'],
+    S(DN, 0): ['xy2', 'own4'], S(DN, 1): ['xy3', 'own5'], S(DN, 2): ['xy4'], S(DN, 3): ['xy5'],
+    S(DN, 4): ['load5'],
 }
 
 
@@ -79,11 +80,6 @@
 
     sib, xn, yn, dn = index(0, 0, 1), index(1, 0, 0), index(0, 1, 0), index(1, 1, 0)
     dev_s, dev_x, dev_y, dev_z = (z, sib), (z, xn), (z, yn), (1 - z, me)
-
-    barrier = pltpu.get_barrier_semaphore()
-    for dev in (dev_s, dev_x, dev_y, dev_z):
-        pl.semaphore_signal(barrier, inc=1, device_id=dev, device_id_type=MESH)
-    pl.semaphore_wait(barrier, 4)
 
     def remote(src, dst, send, recv, dev):
         return pltpu.make_async_remote_copy(src_ref=src, dst_ref=dst, send_sem=send, recv_sem=recv, device_id=dev,
@@ -145,6 +141,8 @@
         elif name[:-1] == 'r':
             rz(k).wait_recv()
             rs(k, core).start()
+        elif name[:-1] == 'load':
+            xstart(xslot[UNITS.index(S(DN, k))], DN, k)
         elif name[:-1] == 'f':
             flush(0, k).wait()
             yz(k).start()
@@ -209,6 +207,7 @@
                 pltpu.make_async_copy(piece(xg.at[c + 1 - core], k), xbuf.at[slot, 1 - core], xsem.at[slot, 1]))
 
     def xstart(slot, rel, k):
+        rel = jnp.int32(rel)
         own, far, sibling = xcopies(slot, rel, k)
 
         @pl.when(rel == OWN)
@@ -262,11 +261,15 @@
             return carry
         lax.fori_loop(0, rows // 16, body, 0, unroll=2)
 
-    for k in range(2):
-        send(0, k).start()
     lcopies(OWN, 'start')
     for k in range(2):
         xcopies(k, OWN, k)[0].start()
+    barrier = pltpu.get_barrier_semaphore()
+    for dev in (dev_s, dev_x, dev_y, dev_z):
+        pl.semaphore_signal(barrier, inc=1, device_id=dev, device_id_type=MESH)
+    pl.semaphore_wait(barrier, 4)
+    for k in range(2):
+        send(0, k).start()
     run('own0')
     for bt in range(nb):
         rz(bt).start()
@@ -336,9 +339,6 @@
 
         @pl.when(kind == 0)
         def _():
-            @pl.when(late_ == 1)
-            def _():
-                xstart(xs_, a0, a1)
             @pl.when(i == 1)
             def _():
                 xcopies(1, OWN, 1)[0].wait()

time: 604 us -> 600 us (level)
  no operation moved by 1% of the time
where the time goes in v3:
time: 600 us
  Pallas kernels  591 us (98%)
  local copies, waits for them, and re-layouts  8.54 us (1%)
    pallas_call x1, Pallas kernels, apply_local(): pl.pallas_call(kernel, out_shape=[shape(x.shape, F32), shape((8,) + x.sha...  591 us

profile of v3, /device:TPU:0, one launch (start us, length us, event | category | flops | bytes accessed | tf_op | source)
XLA Modules:
  0.0 599.8 jit_solution(15926346781739097851)
XLA Ops:
  0.0 591.2 %heff.1 = (f32[384,2,2,1536]{3,2,1,0:T(2,128)}, f32[8,384,2,2,1536]{4,3,2,1,0:T(2,128)}, f32[3,1536,1536]{2,1,0:T(8,128)}, f32[3,4,384,512]{3,2,1,0:T(8,128)}, f...) custom-call(f32[384,2,2,1536]{3,2,1,0:T(2,128)} %x_ref.1, f32[3,384,3072]{2,1,0:T(8,128)} %bitcast.3, ...), custom_call_target="tpu_custom_call" | custom-call | tf_op jit(solution)/shard_map/heff/pallas_call | solution.py:483
  591.2 8.5 %copy.6 = f32[384,2,2,1536]{3,2,1,0:T(2,128)} copy(f32[384,2,2,1536]{3,2,1,0:T(2,128)} %get-tuple-element.6) | data formatting | bytes 18874368

commit v4 on v3

--- a/solution.py
+++ b/solution.py
@@ -22,21 +22,22 @@
     return ('t', own, bt, pair)
 
 
-UNITS = [S(OWN, 0), S(OWN, 1), S(OWN, 2), S(OWN, 3), S(OWN, 4), S(XN, 0), S(YN, 0), S(OWN, 5), S(XN, 1), S(DN, 0), S(YN, 1)]
-UNITS += [S(XN, 2), S(YN, 2), S(DN, 1), Q(0, 0, 0), S(XN, 3), S(YN, 3), S(DN, 2), Q(0, 1, 0), S(XN, 4), S(YN, 4), S(DN, 3)]
+UNITS = [S(OWN, 0), S(OWN, 1), S(OWN, 2), S(OWN, 3), S(OWN, 4), S(XN, 0), S(YN, 0), S(OWN, 5), S(XN, 1), S(YN, 1), S(DN, 0)]
+UNITS += [S(XN, 2), S(YN, 2), S(DN, 1), Q(0, 0, 0), S(XN, 3), S(YN, 3), S(DN, 2), S(XN, 4), Q(0, 1, 0), S(YN, 4), S(DN, 3)]
 UNITS += [Q(0, 0, 1), S(XN, 5), S(YN, 5), S(DN, 4), S(DN, 5), Q(0, 0, 2)]
 UNITS += [Q(0, 1, 1), Q(0, 1, 2)] + [Q(0, 2, pair) for pair in range(3)]
 UNITS += [Q(1, bt, pair) for bt in range(3) for pair in range(3)]
+HALFWAY = {S(DN, 0), S(DN, 2)}
 MIX_AFTER = {S(DN, k): k for k in range(6)}
-LATE = {S(DN, 5)}
+LATE = {S(DN, 5), S(XN, 2), S(XN, 4)}
 AT = {
-    S(OWN, 3): ['xy0', 'own2'], S(YN, 0): ['xy1', 'own3'], S(OWN, 5): ['d0'], S(YN, 1): ['r0'],
-    S(XN, 2): ['d1'], S(XN, 3): ['d2'], S(YN, 3): ['r1'], S(XN, 4): ['d3'], S(XN, 5): ['d4'],
+    S(OWN, 3): ['xy0', 'own2'], S(YN, 0): ['xy1', 'own3'], S(XN, 1): ['d0'], S(DN, 0): ['r0'],
+    S(XN, 2): ['d1'], S(XN, 3): ['d2'], S(DN, 2): ['r1'], Q(0, 1, 0): ['d3'], S(XN, 5): ['d4'],
     S(DN, 4): ['d5'], S(DN, 5): ['r2'],
 }
 MID = {
     S(DN, 0): ['xy2', 'own4'], S(DN, 1): ['xy3', 'own5'], S(DN, 2): ['xy4'], S(DN, 3): ['xy5'],
-    S(DN, 4): ['load5'],
+    S(DN, 4): ['load'],
 }
 
 
@@ -141,8 +142,6 @@
         elif name[:-1] == 'r':
             rz(k).wait_recv()
             rs(k, core).start()
-        elif name[:-1] == 'load':
-            xstart(xslot[UNITS.index(S(DN, k))], DN, k)
         elif name[:-1] == 'f':
             flush(0, k).wait()
             yz(k).start()
@@ -414,14 +413,23 @@
                     @pl.when(i == j)
                     def _():
                         for name in mid[j]:
-                            run(name)
+                            if name == 'load':
+                                xstart(xslot[j + 1], *UNITS[j + 1][1:])
+                            else:
+                                run(name)
 
         @pl.when(mixa_ > 0)
         def _():
             def body(j, carry):
                 mix8(mixa_ - 1, j * 8)
                 return carry
-            lax.fori_loop(0, rows // 8, body, 0, unroll=4)
+            lax.fori_loop(0, rows // 16, body, 0, unroll=4)
+            for j in range(n):
+                if UNITS[j] in HALFWAY:
+                    @pl.when(i == j)
+                    def _():
+                        xstart(xslot[j + 1], *UNITS[j + 1][1:])
+            lax.fori_loop(rows // 16, rows // 8, body, 0, unroll=4)
 
         @pl.when(kind == 1)
         def _():

time: 600 us -> 598 us (level)
  no operation moved by 1% of the time
where the time goes in v4:
time: 598 us; the launch traced here: 597 us
  Pallas kernels  589 us (98%)
  local copies, waits for them, and re-layouts  8.54 us (1%)
    pallas_call x1, Pallas kernels, apply_local(): pl.pallas_call(kernel, out_shape=[shape(x.shape, F32), shape((8,) + x.sha...  589 us

profile of v4, /device:TPU:0, one launch (start us, length us, event | category | flops | bytes accessed | tf_op | source)
XLA Modules:
  0.0 597.4 jit_solution(4649614761645070914)
XLA Ops:
  0.0 588.8 %heff.1 = (f32[384,2,2,1536]{3,2,1,0:T(2,128)}, f32[8,384,2,2,1536]{4,3,2,1,0:T(2,128)}, f32[3,1536,1536]{2,1,0:T(8,128)}, f32[3,4,384,512]{3,2,1,0:T(8,128)}, f...) custom-call(f32[384,2,2,1536]{3,2,1,0:T(2,128)} %x_ref.1, f32[3,384,3072]{2,1,0:T(8,128)} %bitcast.3, ...), custom_call_target="tpu_custom_call" | custom-call | tf_op jit(solution)/shard_map/heff/pallas_call | solution.py:491
  588.8 8.5 %copy.6 = f32[384,2,2,1536]{3,2,1,0:T(2,128)} copy(f32[384,2,2,1536]{3,2,1,0:T(2,128)} %get-tuple-element.6) | data formatting | bytes 18874368
